TPU v7x, 32 devices: a whole 2x2x4 slice. The times are simulated.
32 devices in a mesh: gx: 4 (over y, core), gy: 8 (over z, x).
Axes of the slice: x: 2, y: 2, z: 4, core: 2. Of those that a mesh axis runs over, the one named last changes fastest.
Arguments:
- thermal_anomaly: float32 [32, 128, 1024], P(None, 'gx', 'gy'), may hold values from -6 to 6
- ambient_diffusion: bfloat16 [128, 1024], P('gx', 'gy'), may hold values from 0.019897461 to 0.25
- solar_light: bfloat16 [128, 1024], P('gx', 'gy'), may hold values from 0.5 to 4
- sea_tile_flags: int32 [4, 8, 64], P('gx', 'gy'), may hold values 0 or 1
- flooded_layer_tally: int32 [4, 8, 64], P('gx', 'gy'), may hold values from 1 to 32
- tile_holder_rank: int32 [4, 8, 64, 1], P('gx', 'gy'), may hold values from 0 to 7; in each aligned block of 64 rows (0 to 63, 64 to 127, ..., all dimensions but the last counted through in order) at most 16 rows name the same one
- solute_amounts: float32 [4, 8, 128, 8, 2048], P('gx', 'gy'), may hold values from 0.09 to 11
- reaction_rates: float32 [8, 8], replicated, may hold values from -0.2 to 0.5
Outputs:
- thermal_final: float32 [32, 128, 1024], P(None, 'gx', 'gy')
- solute_final: float32 [4, 8, 128, 8, 2048], P('gx', 'gy')
Inputs may be any that keep to these rules, and one draw needn't show every extreme that they name: `tile_holder_rank`: among the 64 blocks of one device, at most 16 name the same owner, a bound that some block reaches of them.
All inputs are finite; a program needn't handle non-finite values. No bound on the sum of `sea_tile_flags` on one device may be relied on, other than what follows from the above.
Results may differ from a plain program's by a relative error of at most 0.0003.
Values may be sent and summed in bfloat16 or wider, within the bound.
No kernel may reach another device: no remote copies, remote signals or barrier semaphores. Data moves between devices by JAX's collectives and lax.ppermute only.
A program may use at most 128 MiB of HBM per device.

v0:
```python
import jax
import jax.numpy as jnp
from jax import lax
from jax.sharding import PartitionSpec as P

NU_COEF = 0.2
STEP_DT = 0.05
ATTEN_WATER = 0.06
ATTEN_CHL = 0.05
WARMING_SCALE = 0.5
GROWTH_TEMP = 0.063


def with_halo(cells, sides, width):
    for axis, dim in sides:
        count = lax.axis_size(axis)
        ends = count - 1
        head = lax.slice_in_dim(cells, 0, width, axis=dim)
        tail = lax.slice_in_dim(cells, cells.shape[dim] - width, cells.shape[dim], axis=dim)
        cells = jnp.concatenate(
            [
                lax.ppermute(tail, axis, [(i, (i + 1) % count) for i in range(ends)]),
                cells,
                lax.ppermute(head, axis, [((i + 1) % count, i) for i in range(ends)]),
            ],
            axis=dim,
        )
    return cells


def masked_step(field, within_layer):
    center = field[:, 1:-1, 1:-1]
    span_east = center.shape[1]
    span_north = center.shape[2]
    total = jnp.zeros_like(center)
    for first, second in ((0, 1), (2, 1), (1, 0), (1, 2)):
        near = field[:, first : first + span_east, second : second + span_north]
        total = total + within_layer[:, first : first + span_east, second : second + span_north] * (
            near - center
        )
    return center + NU_COEF * within_layer[:, 1:-1, 1:-1] * total


def level_below(values):
    return jnp.concatenate([values[..., 64:], values[..., -64:]], axis=-1)


def level_above_zero(values):
    return jnp.concatenate([jnp.zeros_like(values[..., :64]), values[..., :-64]], axis=-1)


def level_prefix(values, layer_tally):
    running = values
    reach = 1
    while reach < layer_tally:
        moved = jnp.concatenate(
            [jnp.zeros_like(running[..., : 64 * reach]), running[..., : -64 * reach]], axis=-1
        )
        running = running + moved
        reach = reach * 2
    return running


def spread_levels(column_values, layer_tally):
    return jnp.tile(column_values, (1, layer_tally))


def flat_mixer(temp_flat, kbg_flat):
    return (kbg_flat * (1.0 + 0.5 * jnp.tanh(temp_flat - level_below(temp_flat)))).astype(
        jnp.bfloat16
    )


def flat_validity(tile_amount, flat_width):
    levels = lax.broadcasted_iota(jnp.int32, (1, flat_width), 1) // 64
    valid = (levels < tile_amount[:, None]).astype(jnp.float32)
    active = (levels + 1 < tile_amount[:, None]).astype(jnp.float32)
    return (valid, active)


def totals(amounts_on_chip, valid):
    return jnp.sum(amounts_on_chip * valid[:, None], axis=(0, 2))


def column_step(
    temp_flat, kappa_flat, surface, valid, active, amounts_on_chip, reaction_rates, layer_tally
):
    atten = ATTEN_WATER + ATTEN_CHL * amounts_on_chip[:, 0]
    cumul = level_prefix(atten, layer_tally)
    top = surface * jnp.exp(-(cumul - atten))
    bottom = surface * jnp.exp(-cumul)
    heat = (valid * (top - bottom)).astype(jnp.bfloat16)
    growth = jnp.exp(GROWTH_TEMP * temp_flat.astype(jnp.float32)) * top / (top + 1.0)
    mixed = jnp.einsum(
        "rs,nsf->nrf", reaction_rates, amounts_on_chip, precision=lax.Precision.HIGHEST
    )
    flux = (kappa_flat.astype(jnp.float32) * active)[:, None] * (
        level_below(amounts_on_chip) - amounts_on_chip
    )
    new = amounts_on_chip + valid[:, None] * STEP_DT * (
        flux - level_above_zero(flux) + growth[:, None] * mixed
    )
    return (new, heat)


def plane_blocks(field, blocks_x, blocks_y):
    return (
        field.reshape(blocks_x, 8, blocks_y, 8)
        .transpose(0, 2, 1, 3)
        .reshape(blocks_x * blocks_y, 64)
    )


def on_device(
    thermal_anomaly,
    ambient_diffusion,
    solar_light,
    sea_tile_flags,
    flooded_layer_tally,
    tile_holder_rank,
    solute_amounts,
    reaction_rates,
):
    layer_tally = thermal_anomaly.shape[0]
    span_east = thermal_anomaly.shape[1]
    span_north = thermal_anomaly.shape[2]
    blocks_x = span_east // 8
    blocks_y = span_north // 8
    tile_summation = blocks_x * blocks_y
    flat_width = layer_tally * 64
    depth_block = (sea_tile_flags * flooded_layer_tally).reshape(tile_summation)
    cell_count = jnp.repeat(
        jnp.repeat(depth_block.reshape(blocks_x, blocks_y), 8, axis=0), 8, axis=1
    )
    level_idx = lax.broadcasted_iota(jnp.int32, (layer_tally, 1, 1), 0)
    within_layer = (level_idx < cell_count[None]).astype(jnp.float32)
    piled_tiles = jnp.stack([thermal_anomaly, within_layer])
    padded = with_halo(piled_tiles, (("gx", 2), ("gy", 3)), 1)
    advanced_verticals = masked_step(padded[0], padded[1])
    dispatched = advanced_verticals.astype(jnp.bfloat16)
    thermal_tiles = (
        dispatched.reshape(layer_tally, blocks_x, 8, blocks_y, 8)
        .transpose(1, 3, 0, 2, 4)
        .reshape(tile_summation, flat_width)
    )
    ambient_diffusion_tiles = plane_blocks(ambient_diffusion, blocks_x, blocks_y)
    shortwave_blocks = plane_blocks(solar_light, blocks_x, blocks_y)
    diffusion_each_tile = flat_mixer(
        thermal_tiles.astype(jnp.float32),
        spread_levels(ambient_diffusion_tiles.astype(jnp.float32), layer_tally),
    )
    payload = jnp.concatenate([thermal_tiles, diffusion_each_tile, shortwave_blocks], axis=1)
    holder_chip = tile_holder_rank.reshape(tile_summation)
    order = jnp.arange(tile_summation, dtype=jnp.int32)
    same = (holder_chip[:, None] == holder_chip[None, :]) & (order[None, :] < order[:, None])
    rank = jnp.sum(same.astype(jnp.int32), axis=1)
    position_summation = solute_amounts.shape[2]
    device_groups = lax.axis_size("gy")
    slot_limit = position_summation // device_groups
    target_owner = holder_chip * slot_limit + rank
    selection_mask = (
        lax.broadcasted_iota(jnp.int32, (position_summation, tile_summation), 0)
        == target_owner[None, :]
    )
    select_b = selection_mask.astype(jnp.bfloat16)
    packed = jnp.einsum("sb,bf->sf", select_b, payload, preferred_element_type=jnp.float32).astype(
        jnp.bfloat16
    )
    packed_count = jnp.sum(selection_mask.astype(jnp.int32) * depth_block[None, :], axis=1)
    arrived_tiles, received_count = (
        lax.all_to_all(
            packed.reshape(device_groups, slot_limit, packed.shape[1]),
            "gy",
            split_axis=0,
            concat_axis=0,
            tiled=True,
        ),
        lax.all_to_all(
            packed_count.reshape(device_groups, slot_limit),
            "gy",
            split_axis=0,
            concat_axis=0,
            tiled=True,
        ),
    )
    arrived_tiles = arrived_tiles.reshape(position_summation, arrived_tiles.shape[2])
    tile_amount = received_count.reshape(position_summation)
    thermal_at_position = arrived_tiles[:, :flat_width]
    diffusion_at_position = arrived_tiles[:, flat_width : 2 * flat_width]
    solar_at_position = arrived_tiles[:, 2 * flat_width :]
    surface = spread_levels(solar_at_position.astype(jnp.float32), layer_tally)
    amounts_on_chip = solute_amounts.reshape(
        position_summation, solute_amounts.shape[3], flat_width
    )
    valid, active = flat_validity(tile_amount, flat_width)
    old_local = totals(amounts_on_chip, valid)
    cells_local = jnp.sum(valid)
    old_total, cells = lax.psum((old_local, cells_local), ("gx", "gy"))
    new, heat = column_step(
        thermal_at_position,
        diffusion_at_position,
        surface,
        valid,
        active,
        amounts_on_chip,
        reaction_rates,
        layer_tally,
    )
    new_total = lax.psum(totals(new, valid), ("gx", "gy"))
    shift = (old_total - new_total) / jnp.maximum(cells, 1.0)
    solute_final = jnp.where(
        valid[:, None] > 0, new + shift[None, :, None], amounts_on_chip
    ).reshape(solute_amounts.shape)
    returned_blocks = lax.all_to_all(
        heat.reshape(device_groups, slot_limit, flat_width),
        "gy",
        split_axis=0,
        concat_axis=0,
        tiled=True,
    )
    returned_blocks = returned_blocks.reshape(position_summation, flat_width)
    heat_blocks = jnp.einsum(
        "sb,sf->bf", select_b, returned_blocks, preferred_element_type=jnp.float32
    )
    warming_each_site = (
        heat_blocks.reshape(blocks_x, blocks_y, layer_tally, 8, 8)
        .transpose(2, 0, 3, 1, 4)
        .reshape(layer_tally, span_east, span_north)
    )
    thermal_final = advanced_verticals + WARMING_SCALE * warming_each_site
    return (thermal_final, solute_final)


def solution(mesh):
    return jax.shard_map(
        on_device,
        mesh=mesh,
        in_specs=(
            P(None, "gx", "gy"),
            P("gx", "gy"),
            P("gx", "gy"),
            P("gx", "gy", None),
            P("gx", "gy", None),
            P("gx", "gy", None, None),
            P("gx", "gy", None, None, None),
            P(),
        ),
        out_specs=(P(None, "gx", "gy"), P("gx", "gy", None, None, None)),
        check_vma=False,
    )
```

profile of v0, /device:TPU:0, one launch (start us, length us, event | category | flops | bytes accessed | tf_op | source)
XLA Modules:
  0.0 186.1 jit_solution(9731067672512701590)
XLA Ops:
  0.6 0.9 convert_reduce_fusion
  1.6 0.7 multiply_add_fusion
  2.2 0.7 multiply_bitcast_fusion.1
  2.9 0.1 select_reduce_fusion
  3.0 0.7 all_to_all.12
  3.7 7.3 %all-to-all-start = ((s32[8,1,16]{2,1,0:T(1,128)}), s32[8,1,16]{2,1,0:T(1,128)S(1)}, u32[]{:S(2)}, u32[]{:S(2)}) async-start(s32[8,1,16]{2,1,0:T(1,128)} %bitcast.10), calls=%async_computation | async-start | bytes 8192 | tf_op jit(solution)/shard_map/all_to_all | solution.py:178
  11.3 1.2 pad_maximum_fusion.1
  12.5 2.7 %copy.128 = f32[2,32,32,128]{1,3,2,0:T(8,128)} copy(f32[2,32,32,128]{3,2,1,0:T(8,128)S(1)} %pad_maximum_fusion.1) | data formatting | bytes 2097152 | tf_op jit(solution)/shard_map/stack | solution.py:137
  15.2 1.1 fusion.39
  16.3 1.6 collective-permute-start
  17.9 1.3 collective-permute-start.1
  19.2 4.8 %fusion.18 = f32[128,1,2048]{2,1,0:T(1,128)S(1)} fusion(f32[128,8,2048]{2,1,0:T(8,128)} %bitcast.79), kind=kLoop, calls=%fused_computation.37 | loop fusion | flops 524288 | bytes 2097152 | tf_op jit(solution)/shard_map/add | solution.py:88
  24.0 0.3 copy.161
  24.5 0.1 copy.131
  24.6 0.1 copy.132
  24.7 1.3 collective-permute-start.3
  25.9 4.5 %collective-permute-start.2 = (f32[2,32,34,1]{2,1,3,0:T(8,128)S(1)}, f32[2,32,34,1]{2,1,3,0:T(8,128)S(1)}, u32[]{:S(2)}, u32[]{:S(2)}) collective-permute-start(f32[2,32,34,1]{2,1,3,0:T(8,128)S(1)} %copy.131), channel_id=1, source_target_pairs={{0,1},{1,2},{2,3},{3,4},{4,5},{5,6},{6,7},{8,9},{9,10},{10,11},{11... | collective-permute-start | bytes 26120 | tf_op jit(solution)/shard_map/ppermute | solution.py:22
  30.5 0.5 pad_add_fusion.4
  31.0 0.2 reshape.244
  31.2 0.1 copy.138
  31.3 0.7 reshape.245
  32.0 0.2 reshape.253
  32.2 0.1 copy.137
  32.3 0.1 reshape.252
  32.5 0.9 copy.134
  33.3 0.1 copy.133
  33.4 2.7 %pad_maximum_fusion = f32[2,32,34,130]{1,3,2,0:T(8,128)S(1)} fusion(f32[2,32,34,1]{1,3,2,0:T(1,128)S(1)} %copy.134, f32[2,32,1,128]{1,3,2,0:T(8,128)S(1)} %collective-permute-done.1, f32[2,32,32,128]{1,3,2,0:T(8,128)} %copy.128, f32[2,32,1,128]{1,3,2,0:T(8,128)S(1)} %collective-permute-done, f32[2,32,34,1]{1,3,2,0:T(1,128)S(1)} %copy.133), kind=kLoop, calls=%fused_computation.9 | loop fusion | flops 1131520 | bytes 2263040 | tf_op jit(solution)/shard_map/concatenate | solution.py:20
  36.1 0.3 slice_bitcast_fusion
  36.4 3.6 %fusion.37 = (bf16[32,32,128]{0,2,1:T(8,128)(2,1)}, f32[32,32,128]{0,2,1:T(8,128)}) fusion(f32[32,34,130]{0,2,1:T(8,128)S(1)} %get-tuple-element.24, f32[32,34,130]{0,2,1:T(8,128)S(1)} %get-tuple-element.23), kind=kLoop, calls=%fused_computation.87 | loop fusion | flops 1966080 | bytes 6029312 | tf_op jit(solution)/shard_map/convert_element_type | solution.py:140
  40.0 4.9 %copy.136 = bf16[4,16,32,8,8]{1,0,4,3,2:T(4,128)(2,1)S(1)} copy(bf16[4,16,32,8,8]{2,4,1,3,0:T(8,128)(2,1)} %bitcast.87) | data formatting | bytes 524288 | tf_op jit(solution)/shard_map/transpose | solution.py:143
  45.0 1.8 reshape.243
  46.7 0.8 slice.135
  47.5 1.1 slice.134
  48.7 0.3 fusion.23
  48.9 1.5 convolution_convert_fusion
  50.4 2.5 %copy.139 = bf16[128,4160]{1,0:T(8,128)(2,1)} copy(bf16[128,4160]{0,1:T(8,128)(2,1)} %convolution_convert_fusion) | data formatting | bytes 2129920 | tf_op jit(solution)/shard_map/convert_element_type | solution.py:166
  53.0 6.3 %all-to-all-start.1 = ((bf16[8,16,4160]{2,1,0:T(8,128)(2,1)}), bf16[8,16,4160]{2,1,0:T(8,128)(2,1)}, u32[]{:S(2)}, u32[]{:S(2)}) async-start(bf16[8,16,4160]{2,1,0:T(8,128)(2,1)} %bitcast.86), calls=%async_computation.1 | async-start | bytes 2162688 | tf_op jit(solution)/shard_map/all_to_all | solution.py:171
  59.3 0.1 pad_add_fusion.3
  59.4 2.1 %slice.145 = f32[128,8,64]{2,1,0:T(8,128)} slice(f32[128,8,2048]{2,1,0:T(8,128)} %bitcast.80), slice={[0:128], [0:8], [1984:2048]} | slice | bytes 524288 | tf_op jit(solution)/shard_map/slice | solution.py:45
  61.5 9.0 %slice.144 = f32[128,8,1984]{2,1,0:T(8,128)} slice(f32[128,8,2048]{2,1,0:T(8,128)} %bitcast.81), slice={[0:128], [0:8], [64:2048]} | slice | bytes 16252928 | tf_op jit(solution)/shard_map/slice | solution.py:45
  70.5 0.1 pad_add_fusion.2
  70.7 0.1 pad_add_fusion.1
  70.9 0.8 slice.142
  71.8 0.5 broadcast.192
  72.3 0.6 reduce.7
  72.9 1.3 fusion.25
  74.2 12.9 %all-to-all-done.1 = bf16[8,16,4160]{2,1,0:T(8,128)(2,1)} async-done(((bf16[8,16,4160]{2,1,0:T(8,128)(2,1)}), bf16[8,16,4160]{2,1,0:T(8,128)(2,1)}, u32[]{:S(2)}, u32[]{:S(2)}) %all-to-all-start.1) | async-done | bytes 1064992 | tf_op jit(solution)/shard_map/all_to_all | solution.py:171
  87.1 0.8 slice.136
  87.9 0.1 copy.149
  88.0 0.1 tile.20
  88.1 1.4 copy.141
  89.5 4.6 %add_divide_fusion = (f32[128,2048]{1,0:T(8,128)S(1)}, bf16[128,2048]{1,0:T(8,128)(2,1)}, f32[128,2048]{1,0:T(8,128)}, f32[]{:T(128)}, f32[128,2048]{1,0:T(8,128)}) fusion(f32[128,2048]{1,0:T(8,128)} %copy.141, f32[128,2048]{1,0:T(8,128)S(1)} %pad_add_fusion.1, f32[128,1024]{1,0:T(8,128)} %slice.142, bf16[128,4160]{1,0:T(8,128)(2,1)} %bitcast.17, ...), kind=kLoop, calls=%fused_computation.46 | loop fusion | flops 5505023 | bytes 8405508 | tf_op jit(solution)/shard_map/div | solution.py:93
  94.1 3.7 %all-to-all-start.2 = ((bf16[8,16,2048]{2,1,0:T(8,128)(2,1)}), bf16[8,16,2048]{2,1,0:T(8,128)(2,1)S(1)}, u32[]{:S(2)}, u32[]{:S(2)}) async-start(bf16[8,16,2048]{2,1,0:T(8,128)(2,1)} %bitcast.90), calls=%async_computation.2 | async-start | bytes 1048576 | tf_op jit(solution)/shard_map/all_to_all | solution.py:214
  97.9 11.1 %fusion = f32[128,8,2048]{2,1,0:T(8,128)} fusion(f32[128,8,64]{2,1,0:T(8,128)} %slice.145, f32[128,8,1984]{2,1,0:T(8,128)} %slice.144, f32[128,2048]{1,0:T(8,128)} %get-tuple-element.31, f32[1,1,128,8,2048]{4,3,2,1,0:T(8,128)} %param.14), kind=kLoop, calls=%fused_computation.1 | loop fusion | flops 6291456 | bytes 26214400 | tf_op jit(solution)/shard_map/mul | solution.py:97
  109.0 0.1 copy-done.7
  109.1 21.6 %multiply_reduce_fusion = (f32[8]{0:T(128)S(1)}, f32[8]{0:T(128)S(1)}, f32[128,8,2048]{2,1,0:T(8,128)}) fusion(f32[128,2048]{1,0:T(8,128)S(1)} %copy-done.7, f32[1,1,128,8,2048]{4,3,2,1,0:T(8,128)S(1)} %bitcast.83, f32[8,8]{1,0:T(8,128)S(1)} %copy-done, f32[128,2048]{1,0:T(8,128)S(1)} %get-tuple-element.29, f32[128,8,2048]{2,1,0:T(8,128)} %fusion, ...), kind=kOutput, calls=%fused_computation.6 | convolution fusion | flops 220200944 | bytes 36438336 | tf_op jit(solution)/shard_map/rs,nsf->nrf/dot_general | solution.py:94
  130.8 40.8 %all-reduce.6 = (f32[8]{0:T(128)S(1)}, f32[8]{0:T(128)S(1)}, f32[]{:T(128)}) all-reduce(f32[8]{0:T(128)S(1)} %get-tuple-element.17, f32[8]{0:T(128)S(1)} %get-tuple-element.16, f32[]{:T(128)} %get-tuple-element.32), channel_id=1, replica_groups=mesh['gx'=4,'gy'=8] {'gx','gy'}, use_global_device_ids=true, to_apply=%region_3.4 | all-reduce | flops 17 | bytes 136 | tf_op jit(solution)/shard_map/psum | solution.py:198
  172.2 9.3 %select_bitcast_fusion = f32[1,1,128,8,2048]{4,3,2,1,0:T(8,128)} fusion(f32[128,8,2048]{2,1,0:T(8,128)} %get-tuple-element.38, f32[8]{0:T(128)S(1)} %subtract_divide_fusion, pred[128,2048]{1,0:T(8,128)(4,1)S(1)} %get-tuple-element.34, f32[1,1,128,8,2048]{4,3,2,1,0:T(8,128)} %param.14), kind=kLoop, calls=%fused_computation.5 | loop fusion | flops 4194304 | bytes 25428000 | tf_op jit(solution)/shard_map/reshape | solution.py:213
  181.5 0.3 copy.143
  181.8 1.0 multiply_bitcast_fusion
  182.8 0.9 copy.145
  183.7 0.7 copy-done.4
  184.4 0.3 add.123
  184.6 1.5 copy.146
  (46 shorter events, 0.7 us)
Async XLA Ops:
  0.6 108.4 %copy-start = (f32[8,8]{1,0:T(8,128)S(1)}, f32[8,8]{1,0:T(8,128)}, u32[]{:S(2)}) copy-start(f32[8,8]{1,0:T(8,128)} %param.15) | copy-start | bytes 772
  3.7 49.3 %all-to-all-start = ((s32[8,1,16]{2,1,0:T(1,128)}), s32[8,1,16]{2,1,0:T(1,128)S(1)}, u32[]{:S(2)}, u32[]{:S(2)}) async-start(s32[8,1,16]{2,1,0:T(1,128)} %bitcast.10), calls=%async_computation | async-start | bytes 8192 | tf_op jit(solution)/shard_map/all_to_all | solution.py:178
  15.2 9.2 %copy-start.1 = (f32[2,32,32,128]{1,3,2,0:T(8,128)S(1)}, f32[2,32,32,128]{1,3,2,0:T(8,128)}, u32[]{:S(2)}) copy-start(f32[2,32,32,128]{1,3,2,0:T(8,128)} %copy.128) | copy-start | bytes 3145732
  16.3 8.0 %collective-permute-start = (f32[2,32,1,128]{1,3,2,0:T(8,128)S(1)}, f32[2,32,1,128]{1,3,2,0:T(8,128)S(1)}, u32[]{:S(2)}, u32[]{:S(2)}) collective-permute-start(f32[2,32,1,128]{1,3,2,0:T(8,128)S(1)} %get-tuple-element.27), channel_id=1, source_target_pairs={{0,8},{8,16},{16,24},{1,9},{9,17},{17,25},{2,10},{10,18},{18,26},{... | collective-permute-start | bytes 98312 | tf_op jit(solution)/shard_map/ppermute | solution.py:22
  17.9 6.4 %collective-permute-start.1 = (f32[2,32,1,128]{1,3,2,0:T(8,128)S(1)}, f32[2,32,1,128]{1,3,2,0:T(8,128)S(1)}, u32[]{:S(2)}, u32[]{:S(2)}) collective-permute-start(f32[2,32,1,128]{1,3,2,0:T(8,128)S(1)} %get-tuple-element.28), channel_id=1, source_target_pairs={{8,0},{16,8},{24,16},{9,1},{17,9},{25,17},{10,2},{18,10},{26,18},{... | collective-permute-start | bytes 98312 | tf_op jit(solution)/shard_map/ppermute | solution.py:24
  24.5 6.5 %copy-start.9 = (bf16[32,128]{1,0:T(8,128)(2,1)S(1)}, bf16[32,128]{1,0:T(8,128)(2,1)}, u32[]{:S(2)}) copy-start(bf16[32,128]{1,0:T(8,128)(2,1)} %param.10) | copy-start | bytes 24580
  24.5 7.6 %copy-start.10 = (bf16[32,128]{1,0:T(8,128)(2,1)S(1)}, bf16[32,128]{1,0:T(8,128)(2,1)}, u32[]{:S(2)}) copy-start(bf16[32,128]{1,0:T(8,128)(2,1)} %param.9) | copy-start | bytes 24580
  24.7 7.8 %collective-permute-start.3 = (f32[2,32,34,1]{2,1,3,0:T(8,128)S(1)}, f32[2,32,34,1]{2,1,3,0:T(8,128)}, u32[]{:S(2)}, u32[]{:S(2)}) collective-permute-start(f32[2,32,34,1]{2,1,3,0:T(8,128)S(1)} %copy.132), channel_id=1, source_target_pairs={{1,0},{2,1},{3,2},{4,3},{5,4},{6,5},{7,6},{9,8},{10,9},{11,10},{12... | collective-permute-start | bytes 26120 | tf_op jit(solution)/shard_map/ppermute | solution.py:24
  25.9 7.4 %collective-permute-start.2 = (f32[2,32,34,1]{2,1,3,0:T(8,128)S(1)}, f32[2,32,34,1]{2,1,3,0:T(8,128)S(1)}, u32[]{:S(2)}, u32[]{:S(2)}) collective-permute-start(f32[2,32,34,1]{2,1,3,0:T(8,128)S(1)} %copy.131), channel_id=1, source_target_pairs={{0,1},{1,2},{2,3},{3,4},{4,5},{5,6},{6,7},{8,9},{9,10},{10,11},{11... | collective-permute-start | bytes 26120 | tf_op jit(solution)/shard_map/ppermute | solution.py:22
  31.0 5.1 %copy-start.2 = (f32[128,2048]{1,0:T(8,128)}, f32[128,2048]{1,0:T(8,128)S(1)}, u32[]{:S(2)}) copy-start(f32[128,2048]{1,0:T(8,128)S(1)} %pad_add_fusion.4) | copy-start | bytes 3145732
  46.7 1.9 %copy-start.5 = (bf16[64,2048]{0,1:T(8,128)(2,1)S(1)}, bf16[64,2048]{0,1:T(8,128)(2,1)}, u32[]{:S(2)}) copy-start(bf16[64,2048]{0,1:T(8,128)(2,1)} %reshape.243) | copy-start | bytes 786436
  46.7 2.2 %copy-start.8 = (bf16[64,64]{0,1:T(8,128)(2,1)S(1)}, bf16[64,64]{0,1:T(8,128)(2,1)}, u32[]{:S(2)}) copy-start(bf16[64,64]{0,1:T(8,128)(2,1)} %reshape.245) | copy-start | bytes 24580
  50.4 8.9 %copy-start.3 = (f32[128,2048]{1,0:T(8,128)S(1)}, f32[128,2048]{1,0:T(8,128)}, u32[]{:S(2)}) copy-start(f32[128,2048]{1,0:T(8,128)} %copy-done.2) | copy-start | bytes 3145732
  50.4 8.9 %slice-start.2 = ((f32[128,2048]{1,0:T(8,128)}), f32[128,1920]{1,0:T(8,128)S(1)}, s32[]{:S(2)}) async-start(f32[128,2048]{1,0:T(8,128)} %copy-done.2), calls=%async_computation.5 | async-start | bytes 1966080 | tf_op jit(solution)/shard_map/slice | solution.py:57
  53.0 34.2 %all-to-all-start.1 = ((bf16[8,16,4160]{2,1,0:T(8,128)(2,1)}), bf16[8,16,4160]{2,1,0:T(8,128)(2,1)}, u32[]{:S(2)}, u32[]{:S(2)}) async-start(bf16[8,16,4160]{2,1,0:T(8,128)(2,1)} %bitcast.86), calls=%async_computation.1 | async-start | bytes 2162688 | tf_op jit(solution)/shard_map/all_to_all | solution.py:171
  94.1 87.4 %all-to-all-start.2 = ((bf16[8,16,2048]{2,1,0:T(8,128)(2,1)}), bf16[8,16,2048]{2,1,0:T(8,128)(2,1)S(1)}, u32[]{:S(2)}, u32[]{:S(2)}) async-start(bf16[8,16,2048]{2,1,0:T(8,128)(2,1)} %bitcast.90), calls=%async_computation.2 | async-start | bytes 1048576 | tf_op jit(solution)/shard_map/all_to_all | solution.py:214
  97.8 11.2 %slice-start = ((s8[8388608]{0:T(1024)(128)(4,1)}), s8[4194304]{0:T(1024)(128)(4,1)S(1)}, s32[]{:S(2)}) async-start(s8[8388608]{0:T(1024)(128)(4,1)} %bitcast.82), calls=%async_computation.3 | async-start | bytes 8388608
  97.8 11.2 %slice-start.1 = ((s8[8388608]{0:T(1024)(128)(4,1)}), s8[4194304]{0:T(1024)(128)(4,1)S(1)}, s32[]{:S(2)}) async-start(s8[8388608]{0:T(1024)(128)(4,1)} %bitcast.82), calls=%async_computation.4 | async-start | bytes 8388608
  97.9 11.2 %copy-start.6 = (f32[128,2048]{1,0:T(8,128)S(1)}, f32[128,2048]{1,0:T(8,128)}, u32[]{:S(2)}) copy-start(f32[128,2048]{1,0:T(8,128)} %get-tuple-element.33) | copy-start | bytes 3145732
  97.9 11.3 %copy-start.7 = (f32[128,2048]{1,0:T(8,128)S(1)}, f32[128,2048]{1,0:T(8,128)}, u32[]{:S(2)}) copy-start(f32[128,2048]{1,0:T(8,128)} %get-tuple-element.35) | copy-start | bytes 3145732
  182.8 1.6 copy-start.4
where the time goes:
time: 187 us; the launch traced here: 186 us
  other arithmetic  43 us (23%)
  blocking collectives  40.8 us (22%)
  local copies, waits for them, and re-layouts  37.5 us (20%)
  starting transfers between devices  26.1 us (14%)
  matrix products  24.1 us (13%)
  waiting for transfers between devices  12.9 us (7%)
    psum x1, blocking collectives, on_device(): old_total, cells = lax.psum((old_local, cells_local), ('gx', 'gy'))  40.8 us
    dot_general x1, matrix products, column_step(): jnp.einsum('rs,nsf->nrf', reaction_rates, amounts_on_chip, precision=lax....  21.6 us
    slice x4, local copies, waits for them, and re-layouts, level_below(): return jnp.concatenate([values[..., 64:], values[..., -64:]], axis=-1)  13 us
    all_to_all x1, waiting for transfers between devices, on_device(): lax.all_to_all(packed.reshape(device_groups, slot_limit, packed.shape[1])...  12.9 us
    mul x1, other arithmetic, column_step(): (kappa_flat.astype(jnp.float32) * active)[:, None]  11.1 us
    reshape x1, other arithmetic, on_device(): solute_final = jnp.where(valid[:, None] > 0, new + shift[None, :, None],...  9.28 us
    all_to_all x1, starting transfers between devices, on_device(): lax.all_to_all(packed_count.reshape(device_groups, slot_limit), 'gy', spl...  7.28 us
    all_to_all x1, starting transfers between devices, on_device(): lax.all_to_all(packed.reshape(device_groups, slot_limit, packed.shape[1])...  6.32 us
  transfers between devices with their start and end apart: 7, of which 1 were waited for; matrix products, arithmetic and copies ran while one was open for 48% of the time, Pallas kernels for 0%

commit v1 on v0

--- a/solution.py
+++ b/solution.py
@@ -9,6 +9,10 @@
 ATTEN_CHL = 0.05
 WARMING_SCALE = 0.5
 GROWTH_TEMP = 0.063
+
+
+def follow_record(vals, peer_axis, which_axis):
+    return jax.lax.psum(jax.lax.psum(vals, axis_name=peer_axis), axis_name=which_axis)
 
 
 def with_halo(cells, sides, width):
@@ -195,7 +199,7 @@
     valid, active = flat_validity(tile_amount, flat_width)
     old_local = totals(amounts_on_chip, valid)
     cells_local = jnp.sum(valid)
-    old_total, cells = lax.psum((old_local, cells_local), ("gx", "gy"))
+    old_total, cells = follow_record((old_local, cells_local), "gy", "gx")
     new, heat = column_step(
         thermal_at_position,
         diffusion_at_position,

time: 187 us -> 215 us (1.15)
  blocking collectives: 40.8 us -> 68.5 us
    psum x1 -> x3, blocking collectives: 40.8 us -> 68.5 us  [the longest x1 40.3 us: on_device(): new_total = lax.psum(totals(new, valid), ('gx', 'gy'))]
  transfers between devices with their start and end apart: 7 -> 7, of which waited for: 1 -> 1; matrix products, arithmetic and copies ran while one was open for 48% -> 42% of each run, Pallas kernels for 0% -> 0%
where the time goes in v1:
time: 215 us; the launch traced here: 214 us
  blocking collectives  68.5 us (32%)
  other arithmetic  43.1 us (20%)
  local copies, waits for them, and re-layouts  37.4 us (17%)
  starting transfers between devices  26.1 us (12%)
  matrix products  24.1 us (11%)
  waiting for transfers between devices  12.8 us (6%)
    psum x1, blocking collectives, on_device(): new_total = lax.psum(totals(new, valid), ('gx', 'gy'))  40.3 us
    psum x1, blocking collectives, follow_record(): jax.lax.psum(vals, axis_name=peer_axis)  21.7 us
    dot_general x1, matrix products, column_step(): jnp.einsum('rs,nsf->nrf', reaction_rates, amounts_on_chip, precision=lax....  21.6 us
    slice x4, local copies, waits for them, and re-layouts, level_below(): return jnp.concatenate([values[..., 64:], values[..., -64:]], axis=-1)  12.9 us
    all_to_all x1, waiting for transfers between devices, on_device(): lax.all_to_all(packed.reshape(device_groups, slot_limit, packed.shape[1])...  12.8 us
    mul x1, other arithmetic, column_step(): (kappa_flat.astype(jnp.float32) * active)[:, None]  11.1 us
    reshape x1, other arithmetic, on_device(): solute_final = jnp.where(valid[:, None] > 0, new + shift[None, :, None],...  9.28 us
    all_to_all x1, starting transfers between devices, on_device(): lax.all_to_all(packed_count.reshape(device_groups, slot_limit), 'gy', spl...  7.28 us
  transfers between devices with their start and end apart: 7, of which 1 were waited for; matrix products, arithmetic and copies ran while one was open for 42% of the time, Pallas kernels for 0%

profile of v1, /device:TPU:0, one launch (start us, length us, event | category | flops | bytes accessed | tf_op | source)
XLA Modules:
  0.0 213.6 jit_solution(17995508560210853300)
XLA Ops:
  0.6 0.9 convert_reduce_fusion
  1.6 0.7 multiply_add_fusion
  2.2 0.7 multiply_bitcast_fusion.1
  2.9 0.1 select_reduce_fusion
  3.0 0.7 all_to_all.12
  3.7 7.3 %all-to-all-start = ((s32[8,1,16]{2,1,0:T(1,128)}), s32[8,1,16]{2,1,0:T(1,128)S(1)}, u32[]{:S(2)}, u32[]{:S(2)}) async-start(s32[8,1,16]{2,1,0:T(1,128)} %bitcast.10), calls=%async_computation | async-start | bytes 8192 | tf_op jit(solution)/shard_map/all_to_all | solution.py:182
  11.3 1.2 pad_maximum_fusion.1
  12.5 2.7 %copy.128 = f32[2,32,32,128]{1,3,2,0:T(8,128)} copy(f32[2,32,32,128]{3,2,1,0:T(8,128)S(1)} %pad_maximum_fusion.1) | data formatting | bytes 2097152 | tf_op jit(solution)/shard_map/stack | solution.py:141
  15.2 1.1 fusion.39
  16.3 1.6 collective-permute-start
  17.9 1.3 collective-permute-start.1
  19.2 4.8 %fusion.18 = f32[128,1,2048]{2,1,0:T(1,128)S(1)} fusion(f32[128,8,2048]{2,1,0:T(8,128)} %bitcast.79), kind=kLoop, calls=%fused_computation.37 | loop fusion | flops 524288 | bytes 2097152 | tf_op jit(solution)/shard_map/add | solution.py:92
  24.0 0.3 copy.161
  24.5 0.1 copy.131
  24.6 0.1 copy.132
  24.6 1.3 collective-permute-start.3
  25.9 4.5 %collective-permute-start.2 = (f32[2,32,34,1]{2,1,3,0:T(8,128)S(1)}, f32[2,32,34,1]{2,1,3,0:T(8,128)S(1)}, u32[]{:S(2)}, u32[]{:S(2)}) collective-permute-start(f32[2,32,34,1]{2,1,3,0:T(8,128)S(1)} %copy.131), channel_id=1, source_target_pairs={{0,1},{1,2},{2,3},{3,4},{4,5},{5,6},{6,7},{8,9},{9,10},{10,11},{11... | collective-permute-start | bytes 26120 | tf_op jit(solution)/shard_map/ppermute | solution.py:26
  30.5 0.5 pad_add_fusion.4
  31.0 0.2 reshape.244
  31.2 0.1 copy.138
  31.3 0.7 reshape.245
  32.0 0.2 reshape.253
  32.2 0.1 copy.137
  32.3 0.1 reshape.252
  32.5 0.9 copy.134
  33.3 0.1 copy.133
  33.4 2.7 %pad_maximum_fusion = f32[2,32,34,130]{1,3,2,0:T(8,128)S(1)} fusion(f32[2,32,34,1]{1,3,2,0:T(1,128)S(1)} %copy.134, f32[2,32,1,128]{1,3,2,0:T(8,128)S(1)} %collective-permute-done.1, f32[2,32,32,128]{1,3,2,0:T(8,128)} %copy.128, f32[2,32,1,128]{1,3,2,0:T(8,128)S(1)} %collective-permute-done, f32[2,32,34,1]{1,3,2,0:T(1,128)S(1)} %copy.133), kind=kLoop, calls=%fused_computation.9 | loop fusion | flops 1131520 | bytes 2263040 | tf_op jit(solution)/shard_map/concatenate | solution.py:24
  36.1 0.3 slice_bitcast_fusion
  36.4 3.6 %fusion.37 = (bf16[32,32,128]{0,2,1:T(8,128)(2,1)}, f32[32,32,128]{0,2,1:T(8,128)}) fusion(f32[32,34,130]{0,2,1:T(8,128)S(1)} %get-tuple-element.25, f32[32,34,130]{0,2,1:T(8,128)S(1)} %get-tuple-element.24), kind=kLoop, calls=%fused_computation.87 | loop fusion | flops 1966080 | bytes 6029312 | tf_op jit(solution)/shard_map/convert_element_type | solution.py:144
  40.0 4.9 %copy.136 = bf16[4,16,32,8,8]{1,0,4,3,2:T(4,128)(2,1)S(1)} copy(bf16[4,16,32,8,8]{2,4,1,3,0:T(8,128)(2,1)} %bitcast.87) | data formatting | bytes 524288 | tf_op jit(solution)/shard_map/transpose | solution.py:147
  45.0 1.8 reshape.243
  46.7 0.8 slice.135
  47.5 1.1 slice.134
  48.6 0.3 fusion.23
  48.9 1.5 convolution_convert_fusion
  50.4 2.5 %copy.139 = bf16[128,4160]{1,0:T(8,128)(2,1)} copy(bf16[128,4160]{0,1:T(8,128)(2,1)} %convolution_convert_fusion) | data formatting | bytes 2129920 | tf_op jit(solution)/shard_map/convert_element_type | solution.py:170
  53.0 6.3 %all-to-all-start.1 = ((bf16[8,16,4160]{2,1,0:T(8,128)(2,1)}), bf16[8,16,4160]{2,1,0:T(8,128)(2,1)}, u32[]{:S(2)}, u32[]{:S(2)}) async-start(bf16[8,16,4160]{2,1,0:T(8,128)(2,1)} %bitcast.86), calls=%async_computation.1 | async-start | bytes 2162688 | tf_op jit(solution)/shard_map/all_to_all | solution.py:175
  59.3 0.1 pad_add_fusion.3
  59.4 2.0 slice.145
  61.4 9.0 %slice.144 = f32[128,8,1984]{2,1,0:T(8,128)} slice(f32[128,8,2048]{2,1,0:T(8,128)} %bitcast.81), slice={[0:128], [0:8], [64:2048]} | slice | bytes 16252928 | tf_op jit(solution)/shard_map/slice | solution.py:49
  70.5 0.1 pad_add_fusion.2
  70.7 0.1 pad_add_fusion.1
  70.8 0.8 slice.142
  71.7 0.5 broadcast.192
  72.3 0.6 reduce.7
  73.0 1.3 fusion.25
  74.3 12.8 %all-to-all-done.1 = bf16[8,16,4160]{2,1,0:T(8,128)(2,1)} async-done(((bf16[8,16,4160]{2,1,0:T(8,128)(2,1)}), bf16[8,16,4160]{2,1,0:T(8,128)(2,1)}, u32[]{:S(2)}, u32[]{:S(2)}) %all-to-all-start.1) | async-done | bytes 1064992 | tf_op jit(solution)/shard_map/all_to_all | solution.py:175
  87.1 0.8 slice.136
  87.9 0.1 tile.20
  88.1 1.4 copy.141
  89.4 4.6 %add_divide_fusion = (f32[128,2048]{1,0:T(8,128)S(1)}, bf16[128,2048]{1,0:T(8,128)(2,1)}, f32[128,2048]{1,0:T(8,128)}, f32[]{:T(128)}, f32[128,2048]{1,0:T(8,128)}) fusion(f32[128,2048]{1,0:T(8,128)} %copy.141, f32[128,2048]{1,0:T(8,128)S(1)} %pad_add_fusion.1, f32[128,1024]{1,0:T(8,128)} %slice.142, bf16[128,4160]{1,0:T(8,128)(2,1)} %bitcast.17, ...), kind=kLoop, calls=%fused_computation.46 | loop fusion | flops 5505023 | bytes 8405508 | tf_op jit(solution)/shard_map/div | solution.py:97
  94.1 3.8 %all-to-all-start.2 = ((bf16[8,16,2048]{2,1,0:T(8,128)(2,1)}), bf16[8,16,2048]{2,1,0:T(8,128)(2,1)S(1)}, u32[]{:S(2)}, u32[]{:S(2)}) async-start(bf16[8,16,2048]{2,1,0:T(8,128)(2,1)} %bitcast.90), calls=%async_computation.2 | async-start | bytes 1048576 | tf_op jit(solution)/shard_map/all_to_all | solution.py:218
  97.8 11.1 %fusion = f32[128,8,2048]{2,1,0:T(8,128)} fusion(f32[128,8,64]{2,1,0:T(8,128)} %slice.145, f32[128,8,1984]{2,1,0:T(8,128)} %slice.144, f32[128,2048]{1,0:T(8,128)} %get-tuple-element.32, f32[1,1,128,8,2048]{4,3,2,1,0:T(8,128)} %param.14), kind=kLoop, calls=%fused_computation.1 | loop fusion | flops 6291456 | bytes 26214400 | tf_op jit(solution)/shard_map/mul | solution.py:101
  109.0 21.6 %multiply_reduce_fusion = (f32[8]{0:T(128)S(1)}, f32[8]{0:T(128)S(1)}, f32[128,8,2048]{2,1,0:T(8,128)}) fusion(f32[128,2048]{1,0:T(8,128)S(1)} %copy-done.7, f32[1,1,128,8,2048]{4,3,2,1,0:T(8,128)S(1)} %bitcast.83, f32[8,8]{1,0:T(8,128)S(1)} %copy-done, f32[128,2048]{1,0:T(8,128)S(1)} %get-tuple-element.30, f32[128,8,2048]{2,1,0:T(8,128)} %fusion, ...), kind=kOutput, calls=%fused_computation.6 | convolution fusion | flops 220200944 | bytes 36438336 | tf_op jit(solution)/shard_map/rs,nsf->nrf/dot_general | solution.py:98
  130.6 40.3 %psum.37 = f32[8]{0:T(128)S(1)} all-reduce(f32[8]{0:T(128)S(1)} %get-tuple-element.16), channel_id=1, replica_groups=mesh['gx'=4,'gy'=8] {'gx','gy'}, use_global_device_ids=true, to_apply=%region_6.7 | all-reduce | flops 8 | bytes 64 | tf_op jit(solution)/shard_map/psum | solution.py:213
  170.9 21.7 %all-reduce.6 = (f32[8]{0:T(128)S(1)}, f32[]{:T(128)}) all-reduce(f32[8]{0:T(128)S(1)} %get-tuple-element.17, f32[]{:T(128)} %get-tuple-element.33), channel_id=1, replica_groups=mesh['gx'=4,'gy'=8] {'gy'}, use_global_device_ids=true, to_apply=%region_3.4 | all-reduce | flops 9 | bytes 72 | tf_op jit(solution)/shard_map/psum | solution.py:15
  192.6 6.5 %all-reduce.7 = (f32[8]{0:T(128)S(1)}, f32[]{:T(128)}) all-reduce(f32[8]{0:T(128)S(1)} %get-tuple-element.18, f32[]{:T(128)} %get-tuple-element.19), channel_id=1, replica_groups=mesh['gx'=4,'gy'=8] {'gx'}, use_global_device_ids=true, to_apply=%region_4.5 | all-reduce | flops 9 | bytes 72 | tf_op jit(solution)/shard_map/psum | solution.py:15
  199.7 9.3 %select_bitcast_fusion = f32[1,1,128,8,2048]{4,3,2,1,0:T(8,128)} fusion(f32[128,8,2048]{2,1,0:T(8,128)} %get-tuple-element.39, f32[8]{0:T(128)S(1)} %subtract_divide_fusion, pred[128,2048]{1,0:T(8,128)(4,1)S(1)} %get-tuple-element.35, f32[1,1,128,8,2048]{4,3,2,1,0:T(8,128)} %param.14), kind=kLoop, calls=%fused_computation.5 | loop fusion | flops 4194304 | bytes 25428000 | tf_op jit(solution)/shard_map/reshape | solution.py:217
  209.0 0.3 copy.143
  209.3 1.0 multiply_bitcast_fusion
  210.3 0.9 copy.145
  211.2 0.7 copy-done.4
  211.9 0.3 add.127
  212.2 1.5 copy.146
  (48 shorter events, 0.8 us)
Async XLA Ops:
  0.6 108.3 %copy-start = (f32[8,8]{1,0:T(8,128)S(1)}, f32[8,8]{1,0:T(8,128)}, u32[]{:S(2)}) copy-start(f32[8,8]{1,0:T(8,128)} %param.15) | copy-start | bytes 772
  3.7 49.3 %all-to-all-start = ((s32[8,1,16]{2,1,0:T(1,128)}), s32[8,1,16]{2,1,0:T(1,128)S(1)}, u32[]{:S(2)}, u32[]{:S(2)}) async-start(s32[8,1,16]{2,1,0:T(1,128)} %bitcast.10), calls=%async_computation | async-start | bytes 8192 | tf_op jit(solution)/shard_map/all_to_all | solution.py:182
  15.2 9.2 %copy-start.1 = (f32[2,32,32,128]{1,3,2,0:T(8,128)S(1)}, f32[2,32,32,128]{1,3,2,0:T(8,128)}, u32[]{:S(2)}) copy-start(f32[2,32,32,128]{1,3,2,0:T(8,128)} %copy.128) | copy-start | bytes 3145732
  16.3 8.0 %collective-permute-start = (f32[2,32,1,128]{1,3,2,0:T(8,128)S(1)}, f32[2,32,1,128]{1,3,2,0:T(8,128)S(1)}, u32[]{:S(2)}, u32[]{:S(2)}) collective-permute-start(f32[2,32,1,128]{1,3,2,0:T(8,128)S(1)} %get-tuple-element.28), channel_id=1, source_target_pairs={{0,8},{8,16},{16,24},{1,9},{9,17},{17,25},{2,10},{10,18},{18,26},{... | collective-permute-start | bytes 98312 | tf_op jit(solution)/shard_map/ppermute | solution.py:26
  17.9 6.4 %collective-permute-start.1 = (f32[2,32,1,128]{1,3,2,0:T(8,128)S(1)}, f32[2,32,1,128]{1,3,2,0:T(8,128)S(1)}, u32[]{:S(2)}, u32[]{:S(2)}) collective-permute-start(f32[2,32,1,128]{1,3,2,0:T(8,128)S(1)} %get-tuple-element.29), channel_id=1, source_target_pairs={{8,0},{16,8},{24,16},{9,1},{17,9},{25,17},{10,2},{18,10},{26,18},{... | collective-permute-start | bytes 98312 | tf_op jit(solution)/shard_map/ppermute | solution.py:28
  24.4 6.5 %copy-start.9 = (bf16[32,128]{1,0:T(8,128)(2,1)S(1)}, bf16[32,128]{1,0:T(8,128)(2,1)}, u32[]{:S(2)}) copy-start(bf16[32,128]{1,0:T(8,128)(2,1)} %param.10) | copy-start | bytes 24580
  24.5 7.6 %copy-start.10 = (bf16[32,128]{1,0:T(8,128)(2,1)S(1)}, bf16[32,128]{1,0:T(8,128)(2,1)}, u32[]{:S(2)}) copy-start(bf16[32,128]{1,0:T(8,128)(2,1)} %param.9) | copy-start | bytes 24580
  24.6 7.8 %collective-permute-start.3 = (f32[2,32,34,1]{2,1,3,0:T(8,128)S(1)}, f32[2,32,34,1]{2,1,3,0:T(8,128)}, u32[]{:S(2)}, u32[]{:S(2)}) collective-permute-start(f32[2,32,34,1]{2,1,3,0:T(8,128)S(1)} %copy.132), channel_id=1, source_target_pairs={{1,0},{2,1},{3,2},{4,3},{5,4},{6,5},{7,6},{9,8},{10,9},{11,10},{12... | collective-permute-start | bytes 26120 | tf_op jit(solution)/shard_map/ppermute | solution.py:28
  25.9 7.4 %collective-permute-start.2 = (f32[2,32,34,1]{2,1,3,0:T(8,128)S(1)}, f32[2,32,34,1]{2,1,3,0:T(8,128)S(1)}, u32[]{:S(2)}, u32[]{:S(2)}) collective-permute-start(f32[2,32,34,1]{2,1,3,0:T(8,128)S(1)} %copy.131), channel_id=1, source_target_pairs={{0,1},{1,2},{2,3},{3,4},{4,5},{5,6},{6,7},{8,9},{9,10},{10,11},{11... | collective-permute-start | bytes 26120 | tf_op jit(solution)/shard_map/ppermute | solution.py:26
  31.0 5.1 %copy-start.2 = (f32[128,2048]{1,0:T(8,128)}, f32[128,2048]{1,0:T(8,128)S(1)}, u32[]{:S(2)}) copy-start(f32[128,2048]{1,0:T(8,128)S(1)} %pad_add_fusion.4) | copy-start | bytes 3145732
  46.7 1.9 copy-start.5
  46.7 2.2 %copy-start.8 = (bf16[64,64]{0,1:T(8,128)(2,1)S(1)}, bf16[64,64]{0,1:T(8,128)(2,1)}, u32[]{:S(2)}) copy-start(bf16[64,64]{0,1:T(8,128)(2,1)} %reshape.245) | copy-start | bytes 24580
  50.4 8.8 %copy-start.3 = (f32[128,2048]{1,0:T(8,128)S(1)}, f32[128,2048]{1,0:T(8,128)}, u32[]{:S(2)}) copy-start(f32[128,2048]{1,0:T(8,128)} %copy-done.2) | copy-start | bytes 3145732
  50.4 8.8 %slice-start.2 = ((f32[128,2048]{1,0:T(8,128)}), f32[128,1920]{1,0:T(8,128)S(1)}, s32[]{:S(2)}) async-start(f32[128,2048]{1,0:T(8,128)} %copy-done.2), calls=%async_computation.5 | async-start | bytes 1966080 | tf_op jit(solution)/shard_map/slice | solution.py:61
  53.0 34.1 %all-to-all-start.1 = ((bf16[8,16,4160]{2,1,0:T(8,128)(2,1)}), bf16[8,16,4160]{2,1,0:T(8,128)(2,1)}, u32[]{:S(2)}, u32[]{:S(2)}) async-start(bf16[8,16,4160]{2,1,0:T(8,128)(2,1)} %bitcast.86), calls=%async_computation.1 | async-start | bytes 2162688 | tf_op jit(solution)/shard_map/all_to_all | solution.py:175
  94.1 115.0 %all-to-all-start.2 = ((bf16[8,16,2048]{2,1,0:T(8,128)(2,1)}), bf16[8,16,2048]{2,1,0:T(8,128)(2,1)S(1)}, u32[]{:S(2)}, u32[]{:S(2)}) async-start(bf16[8,16,2048]{2,1,0:T(8,128)(2,1)} %bitcast.90), calls=%async_computation.2 | async-start | bytes 1048576 | tf_op jit(solution)/shard_map/all_to_all | solution.py:218
  97.8 11.2 %slice-start = ((s8[8388608]{0:T(1024)(128)(4,1)}), s8[4194304]{0:T(1024)(128)(4,1)S(1)}, s32[]{:S(2)}) async-start(s8[8388608]{0:T(1024)(128)(4,1)} %bitcast.82), calls=%async_computation.3 | async-start | bytes 8388608
  97.8 11.2 %slice-start.1 = ((s8[8388608]{0:T(1024)(128)(4,1)}), s8[4194304]{0:T(1024)(128)(4,1)S(1)}, s32[]{:S(2)}) async-start(s8[8388608]{0:T(1024)(128)(4,1)} %bitcast.82), calls=%async_computation.4 | async-start | bytes 8388608
  97.8 11.2 %copy-start.6 = (f32[128,2048]{1,0:T(8,128)S(1)}, f32[128,2048]{1,0:T(8,128)}, u32[]{:S(2)}) copy-start(f32[128,2048]{1,0:T(8,128)} %get-tuple-element.34) | copy-start | bytes 3145732
  97.8 11.2 %copy-start.7 = (f32[128,2048]{1,0:T(8,128)S(1)}, f32[128,2048]{1,0:T(8,128)}, u32[]{:S(2)}) copy-start(f32[128,2048]{1,0:T(8,128)} %get-tuple-element.36) | copy-start | bytes 3145732
  210.3 1.6 copy-start.4
